TPU v7x, 32 devices: a 4x2x2 block of a 4x4x8 slice. The times are simulated.
32 devices in a mesh: data: 4 (over y, z), expert: 8 (over x, core).
Axes of the slice: x: 4, y: 2, z: 2, core: 2. Of those that a mesh axis runs over, the one named last changes fastest.
The devices are a block of a 4x4x8 slice.
Arguments:
- x: bfloat16 [32768, 2048], P(('data', 'expert')), parts along dimension 0
- idx: int32 [32768, 2], P(('data', 'expert')), parts along dimension 0
- wr: bfloat16 [2048, 8], replicated
- w1: bfloat16 [8, 2048, 5632], P('expert')
- w3: bfloat16 [8, 2048, 5632], P('expert')
- w2: bfloat16 [8, 5632, 2048], P('expert')
Outputs:
- output: bfloat16 [32768, 2048], P(('data', 'expert')), parts along dimension 0
There are 4 independent parts. A program takes and returns all parts, laid end to end along the dimension named above; an argument that names none is the same for every part.
All inputs are finite; a program needn't handle non-finite values.
Results may differ from a plain program's by a relative error of at most 0.00141.
Values are sent between devices in bfloat16 or wider.
A program may use at most 768 MiB of HBM per device.

v0:
```python
import jax
import jax.numpy as jnp
from jax import lax
from jax.sharding import PartitionSpec as P


def _mlp(buf, w1, w3, w2):
    a = jnp.einsum('ecd,edf->ecf', buf, w1, preferred_element_type=jnp.float32)
    b = jnp.einsum('ecd,edf->ecf', buf, w3, preferred_element_type=jnp.float32)
    h = (jax.nn.silu(a) * b).astype(jnp.bfloat16)
    return jnp.einsum('ecf,efd->ecd', h, w2, preferred_element_type=jnp.float32).astype(jnp.bfloat16)


def solution(mesh):
    n = mesh.shape['expert']

    def local(x, idx, wr, w1, w3, w2):
        t, d = x.shape
        k = idx.shape[1]
        e_all = wr.shape[1]
        epd = w1.shape[0]
        cs = 2 * k * t // e_all
        p = t * k
        rows = e_all * cs
        logits = jnp.dot(x, wr, preferred_element_type=jnp.float32)
        ids = jnp.arange(e_all, dtype=jnp.int32)
        g = jax.nn.softmax(jnp.sum(jnp.where(idx[:, :, None] == ids, logits[:, None, :], 0.0), axis=2), axis=-1)
        e = idx.reshape(-1)
        oh = e[:, None] == ids[None, :]
        q = jnp.arange(p, dtype=jnp.int32)
        tri = (q[None, :] <= q[:, None]).astype(jnp.bfloat16)
        cnt = jnp.dot(tri, oh.astype(jnp.bfloat16), preferred_element_type=jnp.float32)
        pos = jnp.sum(jnp.where(oh, cnt, 0.0), axis=1).astype(jnp.int32) - 1
        valid = pos < cs
        dest = jnp.where(valid, e * cs + pos, rows)
        r = jnp.arange(rows, dtype=jnp.int32)
        dm = jnp.any(r[:, None, None] == dest.reshape(t, k)[None], axis=2).astype(x.dtype)
        send = jnp.dot(dm, x, preferred_element_type=x.dtype)
        recv = lax.all_to_all(send, 'expert', 0, 0, tiled=True)
        buf = recv.reshape(n, epd, cs, d).transpose(1, 0, 2, 3).reshape(epd, n * cs, d)
        out = _mlp(buf, w1, w3, w2)
        out = out.reshape(epd, n, cs, d).transpose(1, 0, 2, 3).reshape(n * epd * cs, d)
        back = lax.all_to_all(out, 'expert', 0, 0, tiled=True)
        sel = (dest[:, None] == r[None, :]).astype(x.dtype)
        op = jnp.dot(sel, back, preferred_element_type=back.dtype)
        y = jnp.sum(g[:, :, None] * op.reshape(t, k, d).astype(jnp.float32), axis=1)
        return y.astype(x.dtype)

    tok = P(('data', 'expert'), None)
    wsp = P('expert', None, None)
    return jax.shard_map(local, mesh=mesh, in_specs=(tok, tok, P(), wsp, wsp, wsp), out_specs=tok, check_vma=False)
```

profile of v0, /device:TPU:81, one launch (start us, length us, event | category | flops | bytes accessed | tf_op | source)
XLA Modules:
  0.0 803.8 jit_solution(7846384771204429095)
XLA Ops:
  0.0 0.0 copy-start
  0.0 0.7 broadcast_multiply_fusion
  0.7 0.9 copy.16
  1.6 0.2 copy.18
  1.9 0.3 eq.73
  2.1 1.4 fusion.19
  3.6 0.5 sub.21
  4.1 0.1 add_select_fusion
  4.1 0.2 copy.19
  4.3 0.0 copy-start.2
  4.3 11.3 %fusion.3 = pred[4096,1024]{1,0:T(8,128)(4,1)} fusion(s32[1024,2]{0,1:T(2,128)S(1)} %copy.19), kind=kLoop, calls=%fused_computation.5 | loop fusion | flops 12582912 | bytes 4202496 | tf_op jit(solution)/shard_map/reduce_or | solution.py:37
  15.6 23.8 %fusion.16 = bf16[8,512,2048]{2,1,0:T(8,128)(2,1)} fusion(pred[8,512,1024]{2,1,0:T(8,128)(4,1)} %bitcast.35, bf16[1024,2048]{1,0:T(8,128)(2,1)} %param.6), kind=kOutput, calls=%fused_computation.16 | convolution fusion | flops 17179869184 | bytes 25165824 | tf_op jit(solution)/shard_map/dot_general | solution.py:38
  39.4 0.0 copy-done.2
  39.4 193.4 %all_to_all.21 = bf16[8,512,2048]{2,1,0:T(8,128)(2,1)} all-to-all(bf16[8,512,2048]{2,1,0:T(8,128)(2,1)} %fusion.16), channel_id=1, replica_groups=mesh['data'=4,'expert'=8] {'expert'}, dimensions={0} | all-to-all | bytes 33554432 | tf_op jit(solution)/shard_map/all_to_all | solution.py:39
  232.8 106.4 %fusion.7 = f32[4096,5632]{1,0:T(8,128)} fusion(bf16[4096,2048]{1,0:T(8,128)(2,1)} %bitcast.33, bf16[1,2048,5632]{2,1,0:T(8,128)(2,1)} %param.9), kind=kOutput, calls=%fused_computation.9 | convolution fusion | flops 94489280512 | bytes 132120576 | tf_op jit(solution)/shard_map/ecd,edf->ecf/dot_general | solution.py:8
  339.2 124.9 %multiply_convert_fusion = bf16[4096,5632]{1,0:T(8,128)(2,1)} fusion(f32[4096,5632]{1,0:T(8,128)} %fusion.7, bf16[4096,2048]{1,0:T(8,128)(2,1)} %bitcast.34, bf16[1,2048,5632]{2,1,0:T(8,128)(2,1)} %param.10), kind=kOutput, calls=%fused_computation | convolution fusion | flops 94627692544 | bytes 178257920 | tf_op jit(solution)/shard_map/ecd,edf->ecf/dot_general | solution.py:9
  464.0 105.5 %fusion.11 = bf16[4096,2048]{1,0:T(8,128)(2,1)} fusion(bf16[4096,5632]{1,0:T(8,128)(2,1)} %multiply_convert_fusion, bf16[1,5632,2048]{2,1,0:T(8,128)(2,1)} %param.11), kind=kOutput, calls=%fused_computation.15 | convolution fusion | flops 94497669120 | bytes 85983232 | tf_op jit(solution)/shard_map/ecf,efd->ecd/dot_general | solution.py:11
  569.6 0.0 copy-start.1
  569.6 0.0 copy-start.3
  569.6 7.3 all-to-all-start.1
  576.9 0.0 copy-done
  576.9 3.4 fusion.23
  580.3 0.0 copy-done.1
  580.4 179.8 %all-to-all-done.1 = bf16[8,512,2048]{2,1,0:T(8,128)(2,1)} async-done(((bf16[8,512,2048]{2,1,0:T(8,128)(2,1)}), bf16[8,512,2048]{2,1,0:T(8,128)(2,1)}, u32[]{:S(2)}, u32[]{:S(2)}) %all-to-all-start.1) | async-done | bytes 16777248 | tf_op jit(solution)/shard_map/all_to_all | solution.py:43
  760.3 0.0 copy-done.3
  760.3 43.2 %multiply_reduce_fusion = bf16[1024,2048]{1,0:T(8,128)(2,1)} fusion(f32[1024,2]{0,1:T(2,128)S(1)} %fusion.21, bf16[4096,2048,1]{1,0,2:T(8,128)(2,1)} %bitcast.9, s32[1024,2]{0,1:T(2,128)S(1)} %copy-done.3), kind=kOutput, calls=%fused_computation.11 | convolution fusion | flops 34378612736 | bytes 20987904 | tf_op jit(solution)/shard_map/dot_general | solution.py:45
  (5 shorter events, 0.1 us)
Async XLA Ops:
  0.0 576.9 %copy-start = (bf16[2048,8]{0,1:T(8,128)(2,1)S(1)}, bf16[2048,8]{0,1:T(8,128)(2,1)}, u32[]{:S(2)}) copy-start(bf16[2048,8]{0,1:T(8,128)(2,1)} %param.8) | copy-start | bytes 98308
  4.3 35.1 %copy-start.2 = (s32[1024,2]{0,1:T(2,128)}, s32[1024,2]{0,1:T(2,128)S(1)}, u32[]{:S(2)}) copy-start(s32[1024,2]{0,1:T(2,128)S(1)} %copy.19) | copy-start | bytes 24580
  569.6 10.7 %copy-start.1 = (s32[1024,2]{0,1:T(2,128)S(1)}, s32[1024,2]{0,1:T(2,128)}, u32[]{:S(2)}) copy-start(s32[1024,2]{0,1:T(2,128)} %param.7) | copy-start | bytes 24580
  569.6 190.7 %copy-start.3 = (s32[1024,2]{0,1:T(2,128)S(1)}, s32[1024,2]{0,1:T(2,128)}, u32[]{:S(2)}) copy-start(s32[1024,2]{0,1:T(2,128)} %copy-done.2) | copy-start | bytes 24580
  569.6 190.7 %all-to-all-start.1 = ((bf16[8,512,2048]{2,1,0:T(8,128)(2,1)}), bf16[8,512,2048]{2,1,0:T(8,128)(2,1)}, u32[]{:S(2)}, u32[]{:S(2)}) async-start(bf16[8,512,2048]{2,1,0:T(8,128)(2,1)} %bitcast.32), calls=%async_computation.1 | async-start | bytes 33554432 | tf_op jit(solution)/shard_map/all_to_all | solution.py:43
where the time goes:
time: 807 us; the launch traced here: 804 us
  matrix products  409 us (51%)
  blocking collectives  193 us (24%)
  waiting for transfers between devices  180 us (22%)
  other arithmetic  12.2 us (2%)
    all_to_all x1, blocking collectives, local(): recv = lax.all_to_all(send, 'expert', 0, 0, tiled=True)  193 us
    all_to_all x1, waiting for transfers between devices, local(): back = lax.all_to_all(out, 'expert', 0, 0, tiled=True)  180 us
    dot_general x1, matrix products, _mlp(): b = jnp.einsum('ecd,edf->ecf', buf, w3, preferred_element_type=jnp.float32)  125 us
    dot_general x1, matrix products, _mlp(): a = jnp.einsum('ecd,edf->ecf', buf, w1, preferred_element_type=jnp.float32)  106 us
    dot_general x1, matrix products, _mlp(): jnp.einsum('ecf,efd->ecd', h, w2, preferred_element_type=jnp.float32)  106 us
    dot_general x1, matrix products, local(): op = jnp.dot(sel, back, preferred_element_type=back.dtype)  43.2 us
    dot_general x1, matrix products, local(): send = jnp.dot(dm, x, preferred_element_type=x.dtype)  23.8 us
  transfers between devices with their start and end apart: 1, of which 1 were waited for; matrix products, arithmetic and copies ran while one was open for 0% of the time, Pallas kernels for 0%

commit v1 on v0

v1 whole, which is shorter than its diff:
```python
import jax
import jax.numpy as jnp
from jax import lax
from jax.experimental import pallas as pl
from jax.experimental.pallas import tpu as pltpu
from jax.sharding import PartitionSpec as P


VMEM_LIMIT = 67043328
TT = 128


def _params():
    return pltpu.CompilerParams(vmem_limit_bytes=VMEM_LIMIT)


def _dispatch(pos_or_idx, ecol, x, cap, offs, gate=None):
    first = gate is None
    t, d = x.shape
    m = ecol.shape[0]
    bf = jnp.bfloat16

    def kernel(p_ref, e_ref, x_ref, *refs):
        if first:
            pos_ref, beg_ref, *refs = refs
            e = e_ref[...]
            oh = (p_ref[0:1, :] == e) | (p_ref[1:2, :] == e)
            a = lax.broadcasted_iota(jnp.int32, (t, t), 0)
            b = lax.broadcasted_iota(jnp.int32, (t, t), 1)
            tri = jnp.where(a < b, 1.0, 0.0).astype(bf)
            ohb = jnp.where(oh, 1.0, 0.0).astype(bf)
            cnt = jnp.dot(ohb, tri, preferred_element_type=jnp.float32).astype(jnp.int32)
            pos = jnp.where(oh, cnt, -1)
            pos_ref[...] = pos
            ti = lax.broadcasted_iota(jnp.int32, (t, 128), 0)
            tj = lax.broadcasted_iota(jnp.int32, (t, 128), 1) * TT
            before = jnp.where(ti < tj, 1.0, 0.0).astype(bf)
            beg_ref[...] = jnp.dot(ohb, before, preferred_element_type=jnp.float32).astype(jnp.int32)
        else:
            idx_ref, wr_ref, erow_ref, post_ref, g_ref, *refs = refs
            pos = p_ref[...]
            post_ref[...] = pos.T
            logits = jnp.dot(x_ref[...], wr_ref[...], preferred_element_type=jnp.float32)
            ids = lax.broadcasted_iota(jnp.int32, logits.shape, 1)
            i0, i1 = idx_ref[:, 0:1], idx_ref[:, 1:2]
            s0 = jnp.sum(jnp.where(i0 == ids, logits, 0.0), axis=1, keepdims=True)
            s1 = jnp.sum(jnp.where(i1 == ids, logits, 0.0), axis=1, keepdims=True)
            top = jnp.maximum(s0, s1)
            p0, p1 = jnp.exp(s0 - top), jnp.exp(s1 - top)
            den = p0 + p1
            er = erow_ref[...]
            g_ref[...] = jnp.where(i0 == er, p0 / den, jnp.where(i1 == er, p1 / den, 0.0))
        outs, (dm_ref, st_ref, sem) = refs[:-3], refs[-3:]
        over = jnp.max(pos, axis=(0, 1), keepdims=True) >= cap - 1
        flag = jnp.where(over, 1.0, 0.0)
        r = lax.broadcasted_iota(jnp.int32, (cap, t), 0)
        last = lax.broadcasted_iota(jnp.int32, (16, 128), 0) == 15
        copies = []
        for i, o in enumerate(offs):
            slot = i % 2
            if i >= 2:
                copies[i - 2].wait()
            p = pos[o:o + 1, :]
            dm_ref[...] = jnp.where(r == jnp.where(p < cap - 1, p, -1), 1.0, 0.0).astype(bf)
            st_ref[slot] = jnp.dot(dm_ref[...], x_ref[...], preferred_element_type=jnp.float32).astype(bf)
            tail = st_ref[slot, cap - 16:cap, 0:128].astype(jnp.float32)
            st_ref[slot, cap - 16:cap, 0:128] = jnp.where(last, flag, tail).astype(bf)
            copies.append(pltpu.make_async_copy(st_ref.at[slot], outs[i], sem.at[slot]))
            copies[i].start()
        for c in copies[-2:]:
            c.wait()

    vm = pl.BlockSpec(memory_space=pltpu.VMEM)
    hbm = pl.BlockSpec(memory_space=pl.ANY)
    shapes = [jax.ShapeDtypeStruct((cap, d), bf) for _ in offs]
    specs = [hbm] * len(offs)
    if first:
        shapes = [jax.ShapeDtypeStruct((m, t), jnp.int32), jax.ShapeDtypeStruct((m, 128), jnp.int32)] + shapes
        specs = [vm] * 2 + specs
        extra = []
    else:
        shapes = [jax.ShapeDtypeStruct((t, m), jnp.int32), jax.ShapeDtypeStruct((t, m), jnp.float32)] + shapes
        specs = [vm] * 2 + specs
        extra = list(gate)
    return pl.pallas_call(
        kernel,
        in_specs=[vm] * (3 + len(extra)),
        out_specs=specs,
        out_shape=shapes,
        scratch_shapes=[pltpu.VMEM((cap, t), bf), pltpu.VMEM((2, cap, d), bf), pltpu.SemaphoreType.DMA((2,))],
        compiler_params=_params(),
        cost_estimate=pl.CostEstimate(flops=2 * len(offs) * cap * t * d, bytes_accessed=2 * d * (t + len(offs) * cap), transcendentals=0),
    )(pos_or_idx, ecol, x, *extra)


def _ffn(blocks, prev, w1, w3, w2):
    nb = len(blocks)
    cap, d = blocks[0].shape
    ff = w1.shape[-1]
    ft, nt = 512, 256
    s1, s2 = (3, 3) if nb * cap < 512 else (2, 2)
    n1, n2 = ff // ft, d // nt
    bf = jnp.bfloat16

    def kernel(*refs):
        xs = refs[:nb]
        pf_ref, w1h, w3h, w2h = refs[nb:nb + 4]
        os = refs[nb + 4:2 * nb + 4]
        fl_ref, h_ref, wa, wc, xv, ov, sa, sb, sc, sx, so = refs[2 * nb + 4:]

        def c1(i, slot):
            cols = pl.ds(pl.multiple_of(i * ft, ft), ft)
            return (pltpu.make_async_copy(w1h.at[0, :, cols], wa.at[slot, :, 0:ft], sa.at[slot]),
                    pltpu.make_async_copy(w3h.at[0, :, cols], wa.at[slot, :, ft:2 * ft], sb.at[slot]))

        def c2(i, slot):
            cols = pl.ds(pl.multiple_of(i * nt, nt), nt)
            return pltpu.make_async_copy(w2h.at[0, :, cols], wc.at[slot], sc.at[slot])

        def oc(i, q, slot):
            cols = pl.ds(pl.multiple_of(i * nt, nt), nt)
            return pltpu.make_async_copy(ov.at[slot, pl.ds(q * cap, cap)], os[q].at[:, cols], so.at[slot, q])

        cx = [pltpu.make_async_copy(xs[q], xv.at[pl.ds(q * cap, cap)], sx.at[q]) for q in range(nb)]
        for c in (cx[0], *c1(0, 0), *cx[1:]):
            c.start()
        for c in (*cx, *c1(0, 0)):
            c.wait()
        for s in range(1, s1):
            for c in c1(s, s):
                c.start()

        def step1(i, _):
            slot = lax.rem(i, s1)

            @pl.when(i > 0)
            def _():
                for c in c1(i, slot):
                    c.wait()

            for s in range(s2):
                @pl.when(i == n1 - 2 * s2 + 2 * s - 1)
                def _():
                    c2(s, s).start()
            ab = jnp.dot(xv[...], wa[slot], preferred_element_type=jnp.float32)
            a, b = ab[:, :ft], ab[:, ft:]
            h_ref[:, pl.ds(pl.multiple_of(i * ft, ft), ft)] = (jax.nn.silu(a) * b).astype(bf)

            @pl.when(i + s1 < n1)
            def _():
                for c in c1(i + s1, slot):
                    c.start()

            return 0

        lax.fori_loop(0, n1, step1, 0)

        def step2(i, _):
            slot = lax.rem(i, s2)
            oslot = lax.rem(i, 2)
            c2(i, slot).wait()

            @pl.when(i >= 2)
            def _():
                for q in range(nb):
                    oc(i - 2, q, oslot).wait()

            ov[oslot] = jnp.dot(h_ref[...], wc[slot], preferred_element_type=jnp.float32).astype(bf)
            for q in range(nb):
                oc(i, q, oslot).start()

            @pl.when(i + s2 < n2)
            def _():
                c2(i + s2, slot).start()

            return 0

        lax.fori_loop(0, n2, step2, 0)
        fl = pf_ref[...]
        row = lax.broadcasted_iota(jnp.int32, (16, 128), 0)
        for q in range(nb):
            tail = xv[(q + 1) * cap - 16:(q + 1) * cap, 0:128].astype(jnp.float32)
            fl = jnp.maximum(fl, jnp.max(jnp.where(row == 15, tail, 0.0), axis=0, keepdims=True))
        fl_ref[...] = fl
        for i in (n2 - 2, n2 - 1):
            for q in range(nb):
                oc(i, q, i % 2).wait()

    hbm = pl.BlockSpec(memory_space=pl.ANY)
    vm = pl.BlockSpec(memory_space=pltpu.VMEM)
    return pl.pallas_call(
        kernel,
        in_specs=[hbm] * nb + [vm] + [hbm] * 3,
        out_specs=[hbm] * nb + [vm],
        out_shape=[jax.ShapeDtypeStruct((cap, d), bf)] * nb + [jax.ShapeDtypeStruct((8, 128), jnp.float32)],
        scratch_shapes=[
            pltpu.VMEM((nb * cap, ff), bf),
            pltpu.VMEM((s1, d, 2 * ft), bf),
            pltpu.VMEM((s2, ff, nt), bf),
            pltpu.VMEM((nb * cap, d), bf),
            pltpu.VMEM((2, nb * cap, nt), bf),
            pltpu.SemaphoreType.DMA((s1,)),
            pltpu.SemaphoreType.DMA((s1,)),
            pltpu.SemaphoreType.DMA((s2,)),
            pltpu.SemaphoreType.DMA((nb,)),
            pltpu.SemaphoreType.DMA((2, nb)),
        ],
        compiler_params=_params(),
        cost_estimate=pl.CostEstimate(flops=6 * nb * cap * d * ff, bytes_accessed=6 * d * ff, transcendentals=nb * cap * ff),
    )(*blocks, prev, w1, w3, w2)


def _combine(blocks, pos, beg, g, extra, dtype):
    nb = len(blocks)
    cap, d = blocks[0].shape
    t = pos.shape[0]
    nt = 256
    win = TT + 16
    bf = jnp.bfloat16

    def kernel(beg_ref, pos_ref, g_ref, *refs):
        bs = refs[:nb]
        x_ref = refs[nb] if extra is not None else None
        y_ref, s_ref = refs[-2:]

        def first_row(i, o):
            return pl.multiple_of(jnp.minimum(beg_ref[o, i] // 16 * 16, cap - win), 16)

        @pl.when(pl.program_id(0) == 0)
        def _():
            r = lax.broadcasted_iota(jnp.int32, (TT, win), 1)
            for i in range(t // TT):
                for o in range(nb):
                    p = pos_ref[i * TT:(i + 1) * TT, o:o + 1]
                    p = jnp.where(p < cap - 1, p - first_row(i, o), -1)
                    s_ref[i, o] = jnp.where(r == p, 1.0, 0.0).astype(bf)

        for i in range(t // TT):
            rows = slice(i * TT, (i + 1) * TT)
            acc = x_ref[rows, :] if x_ref is not None else None
            for o in range(nb):
                v = jnp.dot(s_ref[i, o], bs[o][pl.ds(first_row(i, o), win), :], preferred_element_type=jnp.float32)
                v = v * g_ref[rows, o:o + 1]
                acc = v if acc is None else acc + v
            y_ref[rows, :] = acc.astype(dtype)

    small = pl.BlockSpec(pos.shape, lambda i: (0, 0))
    bsp = pl.BlockSpec((cap, nt), lambda i: (0, i))
    ysp = pl.BlockSpec((t, nt), lambda i: (0, i))
    args = [beg, pos, g, *blocks] + ([extra] if extra is not None else [])
    return pl.pallas_call(
        kernel,
        grid=(d // nt,),
        in_specs=[pl.BlockSpec(memory_space=pltpu.SMEM), small, small] + [bsp] * nb + ([ysp] if extra is not None else []),
        out_specs=ysp,
        out_shape=jax.ShapeDtypeStruct((t, d), dtype),
        scratch_shapes=[pltpu.VMEM((t // TT, nb, TT, win), bf)],
        compiler_params=_params(),
        cost_estimate=pl.CostEstimate(flops=2 * nb * 256 * t * d, bytes_accessed=2 * nb * cap * d + 8 * t * d, transcendentals=0),
    )(*args)


def solution(mesh):
    n = mesh.shape['expert']
    chips = n // 2
    offsets = [(dc, f) for dc in range(chips) for f in range(2)]

    def target(s, o):
        dc, f = offsets[o]
        return ((s // 2 + dc) % chips) * 2 + (s % 2) * (1 - 2 * f) + f

    out_perm = [[(s, target(s, o)) for s in range(n)] for o in range(n)]
    back_perm = [[(b, a) for a, b in p] for p in out_perm]

    order = sorted((o for o in range(n) if offsets[o][0]), key=lambda o: (offsets[o][0] == chips // 2, offsets[o][1]))
    near = [o for o in order if offsets[o][0] != chips // 2]
    far = [o for o in order if offsets[o][0] == chips // 2]
    steps = [[0], near[:2], far, near[2:], [1]]

    def local(x, idx, wr, w1, w3, w2):
        t, _ = x.shape
        k = idx.shape[1]
        e_all = wr.shape[1]
        cs = 2 * k * t // e_all
        cap = cs * 23 // 32
        me = lax.axis_index('expert')
        eoff = jnp.stack([target(me, o) for o in range(n)]).astype(jnp.int32)

        ecol = eoff[:, None]
        send = [None] * n
        first = near[:2] + [0]
        pos, beg, *b = _dispatch(idx.T, ecol, x, cap, first)
        for o, v in zip(first, b):
            send[o] = v

        def move(v, o, perm):
            return lax.ppermute(v, 'expert', perm[o])

        recv = list(send)
        back = [None] * n
        fl = jnp.zeros((8, 128), jnp.float32)
        for o in near[:2]:
            recv[o] = move(send[o], o, out_perm)
        for i, offs in enumerate(steps):
            *outs, fl = _ffn([recv[o] for o in offs], fl, w1, w3, w2)
            for o, v in zip(offs, outs):
                back[o] = v if o == 0 else move(v, o, back_perm)
            if i == 0:
                rest = far + near[2:] + [1]
                pos, _ = lax.optimization_barrier([pos, fl])
                post, g, *c = _dispatch(pos, ecol, x, cap, rest, (idx, wr, eoff[None, :]))
                for o, v in zip(rest, c):
                    send[o] = v
                for o in far + [1]:
                    recv[o] = move(send[o], o, out_perm)
            if i == 1:
                *ins, _ = lax.optimization_barrier([send[o] for o in near[2:]] + [fl])
                for o, v in zip(near[2:], ins):
                    recv[o] = move(v, o, out_perm)

        over = fl[0, 0] > 0

        def fast(back, pos, beg, g, *_):
            return _combine(back, pos, beg, g, None, x.dtype)

        def slow(back, pos, beg, g, x, eoff, w1, w3, w2):
            low = (cap - 1) // 32 * 32
            ext = cs - low
            rows = e_all * ext
            q = jnp.where((pos >= cap - 1) & (pos < cs), eoff[None, :] * ext + pos - low, rows)
            r = jnp.arange(rows, dtype=jnp.int32)
            dm = jnp.any(r[:, None, None] == q[None], axis=2).astype(x.dtype)
            sb = jnp.dot(dm, x, preferred_element_type=x.dtype)
            rb = lax.all_to_all(sb, 'expert', 0, 0, tiled=True)
            ob, _ = _ffn([rb], jnp.zeros((8, 128), jnp.float32), w1, w3, w2)
            bk = lax.all_to_all(ob, 'expert', 0, 0, tiled=True)
            tail = 0.0
            for o in range(n):
                sel = (q[:, o][:, None] == r[None, :]).astype(x.dtype)
                tail = tail + g[:, o:o + 1] * jnp.dot(sel, bk, preferred_element_type=jnp.float32)
            return _combine(back, pos, beg, g, tail, x.dtype)

        return lax.cond(over, slow, fast, back, post, beg, g, x, eoff, w1, w3, w2)

    tok = P(('data', 'expert'), None)
    wsp = P('expert', None, None)

    return jax.shard_map(local, mesh=mesh, in_specs=(tok, tok, P(), wsp, wsp, wsp), out_specs=tok, check_vma=False)
```

time: 807 us -> 357 us (0.44)
  matrix products: 409 us -> 0 us
  Pallas kernels: 0 us -> 289 us
  blocking collectives: 193 us -> 0 us
  waiting for transfers between devices: 180 us -> 32.3 us
  starting transfers between devices: 7.31 us -> 21.7 us
  other arithmetic: 12.2 us -> 0 us
    dot_general x7 -> x0, matrix products: 409 us -> none  [the longest x1 125 us: _mlp(): b = jnp.einsum('ecd,edf->ecf', buf, w3, preferred_element_type=jnp.float32)]
    pallas_call x0 -> x8, Pallas kernels: none -> 289 us  [the longest x5 249 us: _ffn(): pl.pallas_call(kernel, in_specs=[hbm] * nb + [vm] + [hbm] * 3, out_specs=...]
    all_to_all x1 -> x0, blocking collectives: 193 us -> none  [local(): recv = lax.all_to_all(send, 'expert', 0, 0, tiled=True)]
    all_to_all x1 -> x0, waiting for transfers between devices: 180 us -> none  [local(): back = lax.all_to_all(out, 'expert', 0, 0, tiled=True)]
    ppermute x0 -> x14, waiting for transfers between devices: none -> 32.3 us  [move(): return lax.ppermute(v, 'expert', perm[o])]
    ppermute x0 -> x14, starting transfers between devices: none -> 21.7 us  [move(): return lax.ppermute(v, 'expert', perm[o])]
    reduce_or x1 -> x0, other arithmetic: 11.3 us -> none  [local(): jnp.any(r[:, None, None] == dest.reshape(t, k)[None], axis=2)]
  transfers between devices with their start and end apart: 1 -> 14, of which waited for: 1 -> 2; matrix products, arithmetic and copies ran while one was open for 0% -> 1% of each run, Pallas kernels for 0% -> 75%
where the time goes in v1:
time: 357 us; the launch traced here: 353 us
  Pallas kernels  289 us (81%)
  waiting for transfers between devices  32.3 us (9%)
  starting transfers between devices  21.7 us (6%)
  local copies, waits for them, and re-layouts  6.56 us (2%)
    pallas_call x5, Pallas kernels, _ffn(): pl.pallas_call(kernel, in_specs=[hbm] * nb + [vm] + [hbm] * 3, out_specs=...  249 us
    ppermute x14, waiting for transfers between devices, move(): return lax.ppermute(v, 'expert', perm[o])  32.3 us
    pallas_call x2, Pallas kernels, _dispatch(): pl.pallas_call(kernel, in_specs=[vm] * (3 + len(extra)), out_specs=specs,...  23.8 us
    ppermute x14, starting transfers between devices, move(): return lax.ppermute(v, 'expert', perm[o])  21.7 us
    pallas_call x1, Pallas kernels, _combine(): pl.pallas_call(kernel, grid=(d // nt,), in_specs=[pl.BlockSpec(memory_spa...  16.8 us
  transfers between devices with their start and end apart: 14, of which 2 were waited for; matrix products, arithmetic and copies ran while one was open for 1% of the time, Pallas kernels for 75%

profile of v1, /device:TPU:81, one launch (start us, length us, event | category | flops | bytes accessed | tf_op | source)
XLA Modules:
  0.0 352.6 jit_solution(9019613385314065924)
XLA Ops:
  0.0 0.1 stack.35
  0.1 0.5 copy-done.3
  0.6 0.7 copy.18.e_ref
  1.3 9.3 %shard_map.66 = (s32[8,1024]{1,0:T(8,128)}, s32[8,128]{1,0:T(8,128)}, bf16[368,2048]{1,0:T(8,128)(2,1)}, bf16[368,2048]{1,0:T(8,128)(2,1)}, bf16[368,2048]{1,0:T(8,128)(2,1)}) custom-call(s32[2,1024]{1,0:T(2,128)} %bitcast.31, s32[8,1]{1,0:T(8,128)} %copy.18.e_ref, bf16[1024,2048]{1,0:T(8,128)(2,1)} %x_ref.3), custom_call_target="tpu_custom_call" | custom-call | flops 4630511616 | bytes 8716288 | tf_op jit(solution)/shard_map/pallas_call | solution.py:85
  10.6 2.3 collective-permute-start.1
  12.8 2.0 collective-permute-start.2
  14.8 0.6 broadcast_11_refs_1_.2.refs_1_
  15.4 34.2 %shard_map.67 = (bf16[368,2048]{1,0:T(8,128)(2,1)}, f32[8,128]{1,0:T(8,128)}) custom-call(bf16[368,2048]{1,0:T(8,128)(2,1)} %get-tuple-element.119.refs_0_, f32[8,128]{1,0:T(8,128)} %broadcast_11_refs_1_.2.refs_1_, bf16[1,2048,5632]{2,1,0:T(8,128)(2,1)} %refs_2_.3, bf16[1,2048,5632]{2,1,0:T(8,128)(2,1)} %refs_3_.9, bf16[1,5632,2048]{2,1,0:T(8,128)(2,1)} %refs_4_.9), custom_call_target="tpu_custom_call" | custom-call | flops 25467813888 | bytes 69206016 | tf_op jit(solution)/shard_map/pallas_call | solution.py:191
  49.6 1.7 copy.20.refs_0_
  51.3 1.7 copy.21.refs_1_
  53.1 14.6 %shard_map.68 = (s32[1024,8]{1,0:T(8,128)}, f32[1024,8]{1,0:T(8,128)}, bf16[368,2048]{1,0:T(8,128)(2,1)}, bf16[368,2048]{1,0:T(8,128)(2,1)}, bf16[368,2048]{1,0:...) custom-call(s32[8,1024]{1,0:T(8,128)} %get-tuple-element.121.p_ref, s32[8,1]{1,0:T(8,128)} %copy.18.e_ref, ...), custom_call_target="tpu_custom_call" | custom-call | flops 7717519360 | bytes 11730944 | tf_op jit(solution)/shard_map/pallas_call | solution.py:85
  67.6 1.6 collective-permute-start.5
  69.2 3.1 collective-permute-start.6
  72.3 0.0 collective-permute-start
  72.3 0.0 collective-permute-done.1.refs_0_
  72.3 0.0 collective-permute-done.2.refs_1_
  72.3 60.3 %shard_map.69 = (bf16[368,2048]{1,0:T(8,128)(2,1)}, bf16[368,2048]{1,0:T(8,128)(2,1)}, f32[8,128]{1,0:T(8,128)}) custom-call(bf16[368,2048]{1,0:T(8,128)(2,1)} %collective-permute-done.1.refs_0_, bf16[368,2048]{1,0:T(8,128)(2,1)} %collective-permute-done.2.refs_1_, f32[8,128]{1,0:T(8,128)} %get-tuple-element.120.refs_2_, bf16[1,2048,5632]{2,1,0:T(8,128)(2,1)} %refs_2_.3, ...), custom_call_target="tpu_custom_call" | custom-call | flops 50935627776 | bytes 69206016 | tf_op jit(solution)/shard_map/pallas_call | solution.py:191
  132.6 0.1 collective-permute-start.3
  132.8 2.9 collective-permute-start.4
  135.7 0.9 collective-permute-done.6.refs_1_
  136.6 59.8 %shard_map.70 = (bf16[368,2048]{1,0:T(8,128)(2,1)}, bf16[368,2048]{1,0:T(8,128)(2,1)}, f32[8,128]{1,0:T(8,128)}) custom-call(bf16[368,2048]{1,0:T(8,128)(2,1)} %collective-permute-done.5.refs_0_, bf16[368,2048]{1,0:T(8,128)(2,1)} %collective-permute-done.6.refs_1_, f32[8,128]{1,0:T(8,128)} %get-tuple-element.127.refs_2_, bf16[1,2048,5632]{2,1,0:T(8,128)(2,1)} %refs_2_.3, ...), custom_call_target="tpu_custom_call" | custom-call | flops 50935627776 | bytes 69206016 | tf_op jit(solution)/shard_map/pallas_call | solution.py:191
  196.4 2.6 collective-permute-start.10
  199.0 0.2 collective-permute-start.11
  199.2 2.7 collective-permute-start.8
  201.9 59.9 %shard_map.71 = (bf16[368,2048]{1,0:T(8,128)(2,1)}, bf16[368,2048]{1,0:T(8,128)(2,1)}, f32[8,128]{1,0:T(8,128)}) custom-call(bf16[368,2048]{1,0:T(8,128)(2,1)} %collective-permute-done.3.refs_0_, bf16[368,2048]{1,0:T(8,128)(2,1)} %collective-permute-done.4.refs_1_, f32[8,128]{1,0:T(8,128)} %get-tuple-element.132.refs_2_, bf16[1,2048,5632]{2,1,0:T(8,128)(2,1)} %refs_2_.3, ...), custom_call_target="tpu_custom_call" | custom-call | flops 50935627776 | bytes 69206016 | tf_op jit(solution)/shard_map/pallas_call | solution.py:191
  261.8 34.2 %shard_map.72 = (bf16[368,2048]{1,0:T(8,128)(2,1)}, f32[8,128]{1,0:T(8,128)}) custom-call(bf16[368,2048]{1,0:T(8,128)(2,1)} %collective-permute-done.refs_0_, f32[8,128]{1,0:T(8,128)} %get-tuple-element.133.refs_1_, bf16[1,2048,5632]{2,1,0:T(8,128)(2,1)} %refs_2_.3, bf16[1,2048,5632]{2,1,0:T(8,128)(2,1)} %refs_3_.9, bf16[1,5632,2048]{2,1,0:T(8,128)(2,1)} %refs_4_.9), custom_call_target="tpu_custom_call" | custom-call | flops 25467813888 | bytes 69206016 | tf_op jit(solution)/shard_map/pallas_call | solution.py:191
  296.1 1.3 collective-permute-start.7
  297.4 3.0 collective-permute-start.9
  300.3 1.2 slice.51
  302.2 31.4 %collective-permute-done.13 = bf16[368,2048]{1,0:T(8,128)(2,1)} collective-permute-done((bf16[368,2048]{1,0:T(8,128)(2,1)}, bf16[368,2048]{1,0:T(8,128)(2,1)}, u32[]{:S(2)}, u32[]{:S(2)}) %collective-permute-start.13) | collective-permute-done | bytes 1507360 | tf_op jit(solution)/shard_map/ppermute | solution.py:297
  333.6 17.7 %conditional.1 = (bf16[1024,2048]{1,0:T(8,128)(2,1)}) conditional(s32[]{:T(128)} %bitcast.16, (s32[8,128]{1,0:T(8,128)}, s32[1024,8]{1,0:T(8,128)}, f32[1024,8]{1,0:T(8,128)}, bf16[368,2048]{1,0:T(8,128)(2,1)}, bf16[368,2048]{1,0:T(8,128)(2,1)}, /*index=5*/bf16[368,2048]{1,0:T(8,128)(2,1)}, bf16[368,2048]{1,0:T(8,128)(2,1)}, ...), branch_computations={%region_0.1_spmd, %region_1.3_spmd} | conditional | flops 145553670144 | bytes 304845024 | solution.py:343
  333.6 16.8 %branch_0_fun.1 = bf16[1024,2048]{1,0:T(8,128)(2,1)} custom-call(s32[8,128]{1,0:T(8,128)} %get-tuple-element.62.beg_ref, s32[1024,8]{1,0:T(8,128)} %get-tuple-element.63.pos_ref, f32[1024,8]{1,0:T(8,128)} %get-tuple-element.64.g_ref, bf16[368,2048]{1,0:T(8,128)(2,1)} %get-tuple-element.65.refs_0_, bf16[368,2048]{1,0:T(8,128)(2,1)} %get-tuple-element.66.refs_1_, ...), custom_call_target="tpu_custom_call" | custom-call | flops 8589934592 | bytes 28835840 | tf_op jit(solution)/shard_map/cond/branch_0_fun/pallas_call | solution.py:251
  (13 shorter events, 0.0 us)
Async XLA Ops:
  0.1 0.5 copy-start.3
  10.6 61.7 %collective-permute-start.1 = (bf16[368,2048]{1,0:T(8,128)(2,1)}, bf16[368,2048]{1,0:T(8,128)(2,1)}, u32[]{:S(2)}, u32[]{:S(2)}) collective-permute-start(bf16[368,2048]{1,0:T(8,128)(2,1)} %get-tuple-element.125), channel_id=1, source_target_pairs={{0,2},{1,3},{2,4},{3,5},{4,6},{5,7},{6,0},{7,1},{8,10},{9,11},{10,... | collective-permute-start | bytes 4521992 | tf_op jit(solution)/shard_map/ppermute | solution.py:297
  12.8 59.5 %collective-permute-start.2 = (bf16[368,2048]{1,0:T(8,128)(2,1)}, bf16[368,2048]{1,0:T(8,128)(2,1)}, u32[]{:S(2)}, u32[]{:S(2)}) collective-permute-start(bf16[368,2048]{1,0:T(8,128)(2,1)} %get-tuple-element.126), channel_id=1, source_target_pairs={{0,6},{1,7},{2,0},{3,1},{4,2},{5,3},{6,4},{7,5},{8,14},{9,15},{10,... | collective-permute-start | bytes 4521992 | tf_op jit(solution)/shard_map/ppermute | solution.py:297
  67.6 68.1 %collective-permute-start.5 = (bf16[368,2048]{1,0:T(8,128)(2,1)}, bf16[368,2048]{1,0:T(8,128)(2,1)}, u32[]{:S(2)}, u32[]{:S(2)}) collective-permute-start(bf16[368,2048]{1,0:T(8,128)(2,1)} %get-tuple-element.130), channel_id=1, source_target_pairs={{0,4},{1,5},{2,6},{3,7},{4,0},{5,1},{6,2},{7,3},{8,12},{9,13},{10,... | collective-permute-start | bytes 4521992 | tf_op jit(solution)/shard_map/ppermute | solution.py:297
  69.2 67.4 %collective-permute-start.6 = (bf16[368,2048]{1,0:T(8,128)(2,1)}, bf16[368,2048]{1,0:T(8,128)(2,1)}, u32[]{:S(2)}, u32[]{:S(2)}) collective-permute-start(bf16[368,2048]{1,0:T(8,128)(2,1)} %get-tuple-element.131), channel_id=1, source_target_pairs={{0,5},{1,4},{2,7},{3,6},{4,1},{5,0},{6,3},{7,2},{8,13},{9,12},{10,... | collective-permute-start | bytes 4521992 | tf_op jit(solution)/shard_map/ppermute | solution.py:297
  72.3 189.5 %collective-permute-start = (bf16[368,2048]{1,0:T(8,128)(2,1)}, bf16[368,2048]{1,0:T(8,128)(2,1)}, u32[]{:S(2)}, u32[]{:S(2)}) collective-permute-start(bf16[368,2048]{1,0:T(8,128)(2,1)} %get-tuple-element.122), channel_id=1, source_target_pairs={{0,1},{1,0},{2,3},{3,2},{4,5},{5,4},{6,7},{7,6},{8,9},{9,8},{10,11... | collective-permute-start | bytes 4521992 | tf_op jit(solution)/shard_map/ppermute | solution.py:297
  132.6 66.6 %collective-permute-start.3 = (bf16[368,2048]{1,0:T(8,128)(2,1)}, bf16[368,2048]{1,0:T(8,128)(2,1)}, u32[]{:S(2)}, u32[]{:S(2)}) collective-permute-start(bf16[368,2048]{1,0:T(8,128)(2,1)} %get-tuple-element.128), channel_id=1, source_target_pairs={{0,3},{1,2},{2,5},{3,4},{4,7},{5,6},{6,1},{7,0},{8,11},{9,10},{10,... | collective-permute-start | bytes 4521992 | tf_op jit(solution)/shard_map/ppermute | solution.py:297
  132.8 66.5 %collective-permute-start.4 = (bf16[368,2048]{1,0:T(8,128)(2,1)}, bf16[368,2048]{1,0:T(8,128)(2,1)}, u32[]{:S(2)}, u32[]{:S(2)}) collective-permute-start(bf16[368,2048]{1,0:T(8,128)(2,1)} %get-tuple-element.129), channel_id=1, source_target_pairs={{0,7},{1,6},{2,1},{3,0},{4,3},{5,2},{6,5},{7,4},{8,15},{9,14},{10,... | collective-permute-start | bytes 4521992 | tf_op jit(solution)/shard_map/ppermute | solution.py:297
  196.4 101.0 %collective-permute-start.10 = (bf16[368,2048]{1,0:T(8,128)(2,1)}, bf16[368,2048]{1,0:T(8,128)(2,1)}, u32[]{:S(2)}, u32[]{:S(2)}) collective-permute-start(bf16[368,2048]{1,0:T(8,128)(2,1)} %get-tuple-element.142), channel_id=1, source_target_pairs={{4,0},{5,1},{6,2},{7,3},{0,4},{1,5},{2,6},{3,7},{12,8},{13,9},{14,... | collective-permute-start | bytes 4521992 | tf_op jit(solution)/shard_map/ppermute | solution.py:297
  199.0 98.4 %collective-permute-start.11 = (bf16[368,2048]{1,0:T(8,128)(2,1)}, bf16[368,2048]{1,0:T(8,128)(2,1)}, u32[]{:S(2)}, u32[]{:S(2)}) collective-permute-start(bf16[368,2048]{1,0:T(8,128)(2,1)} %get-tuple-element.143), channel_id=1, source_target_pairs={{5,0},{4,1},{7,2},{6,3},{1,4},{0,5},{3,6},{2,7},{13,8},{12,9},{15,... | collective-permute-start | bytes 4521992 | tf_op jit(solution)/shard_map/ppermute | solution.py:297
  199.2 103.0 %collective-permute-start.12 = (bf16[368,2048]{1,0:T(8,128)(2,1)}, bf16[368,2048]{1,0:T(8,128)(2,1)}, u32[]{:S(2)}, u32[]{:S(2)}) collective-permute-start(bf16[368,2048]{1,0:T(8,128)(2,1)} %get-tuple-element.144), channel_id=1, source_target_pairs={{6,0},{7,1},{0,2},{1,3},{2,4},{3,5},{4,6},{5,7},{14,8},{15,9},{8,1... | collective-permute-start | bytes 4521992 | tf_op jit(solution)/shard_map/ppermute | solution.py:297
  199.2 103.0 %collective-permute-start.8 = (bf16[368,2048]{1,0:T(8,128)(2,1)}, bf16[368,2048]{1,0:T(8,128)(2,1)}, u32[]{:S(2)}, u32[]{:S(2)}) collective-permute-start(bf16[368,2048]{1,0:T(8,128)(2,1)} %get-tuple-element.140), channel_id=1, source_target_pairs={{2,0},{3,1},{4,2},{5,3},{6,4},{7,5},{0,6},{1,7},{10,8},{11,9},{12,... | collective-permute-start | bytes 4521992 | tf_op jit(solution)/shard_map/ppermute | solution.py:297
  296.1 6.2 %collective-permute-start.7 = (bf16[368,2048]{1,0:T(8,128)(2,1)}, bf16[368,2048]{1,0:T(8,128)(2,1)}, u32[]{:S(2)}, u32[]{:S(2)}) collective-permute-start(bf16[368,2048]{1,0:T(8,128)(2,1)} %get-tuple-element.139), channel_id=1, source_target_pairs={{1,0},{0,1},{3,2},{2,3},{5,4},{4,5},{7,6},{6,7},{9,8},{8,9},{11,10... | collective-permute-start | bytes 4521992 | tf_op jit(solution)/shard_map/ppermute | solution.py:297
  297.4 36.2 %collective-permute-start.13 = (bf16[368,2048]{1,0:T(8,128)(2,1)}, bf16[368,2048]{1,0:T(8,128)(2,1)}, u32[]{:S(2)}, u32[]{:S(2)}) collective-permute-start(bf16[368,2048]{1,0:T(8,128)(2,1)} %get-tuple-element.145), channel_id=1, source_target_pairs={{7,0},{6,1},{1,2},{0,3},{3,4},{2,5},{5,6},{4,7},{15,8},{14,9},{9,1... | collective-permute-start | bytes 4521992 | tf_op jit(solution)/shard_map/ppermute | solution.py:297
  297.4 36.2 %collective-permute-start.9 = (bf16[368,2048]{1,0:T(8,128)(2,1)}, bf16[368,2048]{1,0:T(8,128)(2,1)}, u32[]{:S(2)}, u32[]{:S(2)}) collective-permute-start(bf16[368,2048]{1,0:T(8,128)(2,1)} %get-tuple-element.141), channel_id=1, source_target_pairs={{3,0},{2,1},{5,2},{4,3},{7,4},{6,5},{1,6},{0,7},{11,8},{10,9},{13,... | collective-permute-start | bytes 4521992 | tf_op jit(solution)/shard_map/ppermute | solution.py:297

commit v2 on v1

--- a/solution.py
+++ b/solution.py
@@ -37,38 +37,53 @@
             before = jnp.where(ti < tj, 1.0, 0.0).astype(bf)
             beg_ref[...] = jnp.dot(ohb, before, preferred_element_type=jnp.float32).astype(jnp.int32)
         else:
-            idx_ref, wr_ref, erow_ref, post_ref, g_ref, *refs = refs
+            idx_ref, wr_ref, post_ref, g_ref, *refs = refs
             pos = p_ref[...]
             post_ref[...] = pos.T
-            logits = jnp.dot(x_ref[...], wr_ref[...], preferred_element_type=jnp.float32)
-            ids = lax.broadcasted_iota(jnp.int32, logits.shape, 1)
-            i0, i1 = idx_ref[:, 0:1], idx_ref[:, 1:2]
-            s0 = jnp.sum(jnp.where(i0 == ids, logits, 0.0), axis=1, keepdims=True)
-            s1 = jnp.sum(jnp.where(i1 == ids, logits, 0.0), axis=1, keepdims=True)
+            logits = lax.dot_general(wr_ref[...], x_ref[...], (((1,), (1,)), ((), ())), preferred_element_type=jnp.float32)
+            ids = lax.broadcasted_iota(jnp.int32, logits.shape, 0)
+            i0, i1 = idx_ref[0:1, :], idx_ref[1:2, :]
+            s0 = jnp.sum(jnp.where(i0 == ids, logits, 0.0), axis=0, keepdims=True)
+            s1 = jnp.sum(jnp.where(i1 == ids, logits, 0.0), axis=0, keepdims=True)
             top = jnp.maximum(s0, s1)
             p0, p1 = jnp.exp(s0 - top), jnp.exp(s1 - top)
             den = p0 + p1
-            er = erow_ref[...]
-            g_ref[...] = jnp.where(i0 == er, p0 / den, jnp.where(i1 == er, p1 / den, 0.0))
-        outs, (dm_ref, st_ref, sem) = refs[:-3], refs[-3:]
+            e = e_ref[...]
+            g_ref[...] = jnp.where(i0 == e, p0 / den, jnp.where(i1 == e, p1 / den, 0.0)).T
+        outs, (dm_ref, st_ref, posm_ref, sem) = refs[:-4], refs[-4:]
         over = jnp.max(pos, axis=(0, 1), keepdims=True) >= cap - 1
         flag = jnp.where(over, 1.0, 0.0)
         r = lax.broadcasted_iota(jnp.int32, (cap, t), 0)
         last = lax.broadcasted_iota(jnp.int32, (16, 128), 0) == 15
-        copies = []
-        for i, o in enumerate(offs):
-            slot = i % 2
-            if i >= 2:
-                copies[i - 2].wait()
-            p = pos[o:o + 1, :]
-            dm_ref[...] = jnp.where(r == jnp.where(p < cap - 1, p, -1), 1.0, 0.0).astype(bf)
+
+        def copy(i, slot):
+            return pltpu.make_async_copy(st_ref.at[slot], outs[i], sem.at[slot])
+
+        posm_ref[...] = jnp.where(pos < cap - 1, pos, -1)
+
+        def block(i, _):
+            slot = lax.rem(i, 2)
+            o = offs[-1]
+            for j in range(len(offs) - 1):
+                o = jnp.where(i == j, offs[j], o)
+            dm_ref[...] = jnp.where(r == posm_ref[pl.ds(o, 1), :], 1.0, 0.0).astype(bf)
+
+            @pl.when(i >= 2)
+            def _():
+                copy(0, slot).wait()
+
             st_ref[slot] = jnp.dot(dm_ref[...], x_ref[...], preferred_element_type=jnp.float32).astype(bf)
             tail = st_ref[slot, cap - 16:cap, 0:128].astype(jnp.float32)
             st_ref[slot, cap - 16:cap, 0:128] = jnp.where(last, flag, tail).astype(bf)
-            copies.append(pltpu.make_async_copy(st_ref.at[slot], outs[i], sem.at[slot]))
-            copies[i].start()
-        for c in copies[-2:]:
-            c.wait()
+            for j in range(len(offs)):
+                @pl.when(i == j)
+                def _():
+                    copy(j, slot).start()
+            return 0
+
+        lax.fori_loop(0, len(offs), block, 0)
+        for i in range(max(len(offs) - 2, 0), len(offs)):
+            copy(i, i % 2).wait()
 
     vm = pl.BlockSpec(memory_space=pltpu.VMEM)
     hbm = pl.BlockSpec(memory_space=pl.ANY)
@@ -87,7 +102,7 @@
         in_specs=[vm] * (3 + len(extra)),
         out_specs=specs,
         out_shape=shapes,
-        scratch_shapes=[pltpu.VMEM((cap, t), bf), pltpu.VMEM((2, cap, d), bf), pltpu.SemaphoreType.DMA((2,))],
+        scratch_shapes=[pltpu.VMEM((cap, t), bf), pltpu.VMEM((2, cap, d), bf), pltpu.VMEM((m, t), jnp.int32), pltpu.SemaphoreType.DMA((2,))],
         compiler_params=_params(),
         cost_estimate=pl.CostEstimate(flops=2 * len(offs) * cap * t * d, bytes_accessed=2 * d * (t + len(offs) * cap), transcendentals=0),
     )(pos_or_idx, ecol, x, *extra)
@@ -210,7 +225,7 @@
     )(*blocks, prev, w1, w3, w2)
 
 
-def _combine(blocks, pos, beg, g, extra, dtype):
+def _combine(blocks, pos, beg, g, extra, dtype, base, low, high):
     nb = len(blocks)
     cap, d = blocks[0].shape
     t = pos.shape[0]
@@ -224,15 +239,18 @@
         y_ref, s_ref = refs[-2:]
 
         def first_row(i, o):
-            return pl.multiple_of(jnp.minimum(beg_ref[o, i] // 16 * 16, cap - win), 16)
+            return pl.multiple_of(jnp.clip((beg_ref[o, i] - base) // 16 * 16, 0, cap - win), 16)
 
         @pl.when(pl.program_id(0) == 0)
         def _():
             r = lax.broadcasted_iota(jnp.int32, (TT, win), 1)
-            for i in range(t // TT):
+
+            @pl.loop(0, t // TT)
+            def _(i):
+                ps = pos_ref[pl.ds(pl.multiple_of(i * TT, TT), TT), :]
                 for o in range(nb):
-                    p = pos_ref[i * TT:(i + 1) * TT, o:o + 1]
-                    p = jnp.where(p < cap - 1, p - first_row(i, o), -1)
+                    p = ps[:, o:o + 1]
+                    p = jnp.where((p >= low) & (p < high), p - base - first_row(i, o), -1)
                     s_ref[i, o] = jnp.where(r == p, 1.0, 0.0).astype(bf)
 
         for i in range(t // TT):
@@ -278,7 +296,7 @@
     steps = [[0], near[:2], far, near[2:], [1]]
 
     def local(x, idx, wr, w1, w3, w2):
-        t, _ = x.shape
+        t, d = x.shape
         k = idx.shape[1]
         e_all = wr.shape[1]
         cs = 2 * k * t // e_all
@@ -308,7 +326,7 @@
             if i == 0:
                 rest = far + near[2:] + [1]
                 pos, _ = lax.optimization_barrier([pos, fl])
-                post, g, *c = _dispatch(pos, ecol, x, cap, rest, (idx, wr, eoff[None, :]))
+                post, g, *c = _dispatch(pos, ecol, x, cap, rest, (idx.T, wr.T))
                 for o, v in zip(rest, c):
                     send[o] = v
                 for o in far + [1]:
@@ -321,7 +339,7 @@
         over = fl[0, 0] > 0
 
         def fast(back, pos, beg, g, *_):
-            return _combine(back, pos, beg, g, None, x.dtype)
+            return _combine(back, pos, beg, g, None, x.dtype, 0, 0, cap - 1)
 
         def slow(back, pos, beg, g, x, eoff, w1, w3, w2):
             low = (cap - 1) // 32 * 32
@@ -332,13 +350,12 @@
             dm = jnp.any(r[:, None, None] == q[None], axis=2).astype(x.dtype)
             sb = jnp.dot(dm, x, preferred_element_type=x.dtype)
             rb = lax.all_to_all(sb, 'expert', 0, 0, tiled=True)
-            ob, _ = _ffn([rb], jnp.zeros((8, 128), jnp.float32), w1, w3, w2)
-            bk = lax.all_to_all(ob, 'expert', 0, 0, tiled=True)
-            tail = 0.0
-            for o in range(n):
-                sel = (q[:, o][:, None] == r[None, :]).astype(x.dtype)
-                tail = tail + g[:, o:o + 1] * jnp.dot(sel, bk, preferred_element_type=jnp.float32)
-            return _combine(back, pos, beg, g, tail, x.dtype)
+            zero = jnp.zeros((8, 128), jnp.float32)
+            ob = lax.map(lambda v: _ffn([v], zero, w1, w3, w2)[0], rb.reshape(n, ext, d))
+            bk = lax.all_to_all(ob.reshape(rows, d), 'expert', 0, 0, tiled=True).reshape(n, ext, d)
+            tail = [lax.dynamic_index_in_dim(bk, eoff[o], 0, keepdims=False) for o in range(n)]
+            tail = _combine(tail, pos, beg, g, None, jnp.float32, low, cap - 1, cs)
+            return _combine(back, pos, beg, g, tail, x.dtype, 0, 0, cap - 1)
 
         return lax.cond(over, slow, fast, back, post, beg, g, x, eoff, w1, w3, w2)
 

time: 357 us -> 351 us (0.983); the launches traced: 353 us -> 350 us
  waiting for transfers between devices: 32.3 us -> 38 us
    ppermute x14, waiting for transfers between devices: 32.3 us -> 38 us  [move(): return lax.ppermute(v, 'expert', perm[o])]
  transfers between devices with their start and end apart: 14 -> 14, of which waited for: 2 -> 3; matrix products, arithmetic and copies ran while one was open for 1% -> 1% of each run, Pallas kernels for 75% -> 75%
where the time goes in v2:
time: 351 us; the launch traced here: 350 us
  Pallas kernels  290 us (83%)
  waiting for transfers between devices  38 us (11%)
  starting transfers between devices  18.3 us (5%)
    pallas_call x5, Pallas kernels, _ffn(): pl.pallas_call(kernel, in_specs=[hbm] * nb + [vm] + [hbm] * 3, out_specs=...  248 us
    ppermute x14, waiting for transfers between devices, move(): return lax.ppermute(v, 'expert', perm[o])  38 us
    pallas_call x2, Pallas kernels, _dispatch(): pl.pallas_call(kernel, in_specs=[vm] * (3 + len(extra)), out_specs=specs,...  25.3 us
    ppermute x14, starting transfers between devices, move(): return lax.ppermute(v, 'expert', perm[o])  18.3 us
    pallas_call x1, Pallas kernels, _combine(): pl.pallas_call(kernel, grid=(d // nt,), in_specs=[pl.BlockSpec(memory_spa...  17.3 us
  transfers between devices with their start and end apart: 14, of which 3 were waited for; matrix products, arithmetic and copies ran while one was open for 1% of the time, Pallas kernels for 75%

profile of v2, /device:TPU:81, one launch (start us, length us, event | category | flops | bytes accessed | tf_op | source)
XLA Modules:
  0.0 350.5 jit_solution(13846697443532769116)
XLA Ops:
  0.0 0.1 stack.35
  0.1 0.5 copy-done
  0.6 0.7 copy.12.e_ref
  1.2 10.3 %shard_map.66 = (s32[8,1024]{1,0:T(8,128)}, s32[8,128]{1,0:T(8,128)}, bf16[368,2048]{1,0:T(8,128)(2,1)}, bf16[368,2048]{1,0:T(8,128)(2,1)}, bf16[368,2048]{1,0:T(8,128)(2,1)}) custom-call(s32[2,1024]{1,0:T(2,128)} %bitcast.45, s32[8,1]{1,0:T(8,128)} %copy.12.e_ref, bf16[1024,2048]{1,0:T(8,128)(2,1)} %x_ref.3), custom_call_target="tpu_custom_call" | custom-call | flops 4630511616 | bytes 8716288 | tf_op jit(solution)/shard_map/pallas_call | solution.py:100
  11.5 2.3 collective-permute-start.1
  13.8 1.7 collective-permute-start.2
  15.4 0.6 broadcast_13_refs_1_.2.refs_1_
  16.0 34.2 %shard_map.67 = (bf16[368,2048]{1,0:T(8,128)(2,1)}, f32[8,128]{1,0:T(8,128)}) custom-call(bf16[368,2048]{1,0:T(8,128)(2,1)} %get-tuple-element.175.refs_0_, f32[8,128]{1,0:T(8,128)} %broadcast_13_refs_1_.2.refs_1_, bf16[1,2048,5632]{2,1,0:T(8,128)(2,1)} %refs_2_.3, bf16[1,2048,5632]{2,1,0:T(8,128)(2,1)} %refs_3_.9, bf16[1,5632,2048]{2,1,0:T(8,128)(2,1)} %refs_4_.9), custom_call_target="tpu_custom_call" | custom-call | flops 25467813888 | bytes 69206016 | tf_op jit(solution)/shard_map/pallas_call | solution.py:206
  50.2 15.1 %shard_map.68 = (s32[1024,8]{1,0:T(8,128)}, f32[1024,8]{1,0:T(8,128)}, bf16[368,2048]{1,0:T(8,128)(2,1)}, bf16[368,2048]{1,0:T(8,128)(2,1)}, bf16[368,2048]{1,0:...) custom-call(s32[8,1024]{1,0:T(8,128)} %get-tuple-element.177.p_ref, s32[8,1]{1,0:T(8,128)} %copy.12.e_ref, ...), custom_call_target="tpu_custom_call" | custom-call | flops 7717519360 | bytes 11730944 | tf_op jit(solution)/shard_map/pallas_call | solution.py:100
  65.3 1.5 collective-permute-start
  66.8 1.2 collective-permute-start.5
  68.1 2.1 collective-permute-start.6
  70.1 0.0 collective-permute-done.1.refs_0_
  70.1 0.0 collective-permute-done.2.refs_1_
  70.1 59.8 %shard_map.69 = (bf16[368,2048]{1,0:T(8,128)(2,1)}, bf16[368,2048]{1,0:T(8,128)(2,1)}, f32[8,128]{1,0:T(8,128)}) custom-call(bf16[368,2048]{1,0:T(8,128)(2,1)} %collective-permute-done.1.refs_0_, bf16[368,2048]{1,0:T(8,128)(2,1)} %collective-permute-done.2.refs_1_, f32[8,128]{1,0:T(8,128)} %get-tuple-element.176.refs_2_, bf16[1,2048,5632]{2,1,0:T(8,128)(2,1)} %refs_2_.3, ...), custom_call_target="tpu_custom_call" | custom-call | flops 50935627776 | bytes 69206016 | tf_op jit(solution)/shard_map/pallas_call | solution.py:206
  129.9 0.1 collective-permute-start.3
  130.0 2.9 collective-permute-start.4
  132.9 0.0 collective-permute-done.5.refs_0_
  132.9 0.0 collective-permute-start.8
  132.9 3.3 collective-permute-done.6.refs_1_
  136.3 59.8 %shard_map.70 = (bf16[368,2048]{1,0:T(8,128)(2,1)}, bf16[368,2048]{1,0:T(8,128)(2,1)}, f32[8,128]{1,0:T(8,128)}) custom-call(bf16[368,2048]{1,0:T(8,128)(2,1)} %collective-permute-done.5.refs_0_, bf16[368,2048]{1,0:T(8,128)(2,1)} %collective-permute-done.6.refs_1_, f32[8,128]{1,0:T(8,128)} %get-tuple-element.183.refs_2_, bf16[1,2048,5632]{2,1,0:T(8,128)(2,1)} %refs_2_.3, ...), custom_call_target="tpu_custom_call" | custom-call | flops 50935627776 | bytes 69206016 | tf_op jit(solution)/shard_map/pallas_call | solution.py:206
  196.1 1.4 collective-permute-start.10
  197.4 1.5 collective-permute-start.11
  198.9 59.8 %shard_map.71 = (bf16[368,2048]{1,0:T(8,128)(2,1)}, bf16[368,2048]{1,0:T(8,128)(2,1)}, f32[8,128]{1,0:T(8,128)}) custom-call(bf16[368,2048]{1,0:T(8,128)(2,1)} %collective-permute-done.3.refs_0_, bf16[368,2048]{1,0:T(8,128)(2,1)} %collective-permute-done.4.refs_1_, f32[8,128]{1,0:T(8,128)} %get-tuple-element.188.refs_2_, bf16[1,2048,5632]{2,1,0:T(8,128)(2,1)} %refs_2_.3, ...), custom_call_target="tpu_custom_call" | custom-call | flops 50935627776 | bytes 69206016 | tf_op jit(solution)/shard_map/pallas_call | solution.py:206
  258.8 34.2 %shard_map.72 = (bf16[368,2048]{1,0:T(8,128)(2,1)}, f32[8,128]{1,0:T(8,128)}) custom-call(bf16[368,2048]{1,0:T(8,128)(2,1)} %collective-permute-done.refs_0_, f32[8,128]{1,0:T(8,128)} %get-tuple-element.189.refs_1_, bf16[1,2048,5632]{2,1,0:T(8,128)(2,1)} %refs_2_.3, bf16[1,2048,5632]{2,1,0:T(8,128)(2,1)} %refs_3_.9, bf16[1,5632,2048]{2,1,0:T(8,128)(2,1)} %refs_4_.9), custom_call_target="tpu_custom_call" | custom-call | flops 25467813888 | bytes 69206016 | tf_op jit(solution)/shard_map/pallas_call | solution.py:206
  293.0 0.7 collective-permute-start.7
  293.7 3.0 collective-permute-start.9
  296.7 1.2 slice.3
  298.6 30.7 %collective-permute-done.9 = bf16[368,2048]{1,0:T(8,128)(2,1)} collective-permute-done((bf16[368,2048]{1,0:T(8,128)(2,1)}, bf16[368,2048]{1,0:T(8,128)(2,1)}, u32[]{:S(2)}, u32[]{:S(2)}) %collective-permute-start.9) | collective-permute-done | bytes 1507360 | tf_op jit(solution)/shard_map/ppermute | solution.py:315
  329.2 4.0 %collective-permute-done.13 = bf16[368,2048]{1,0:T(8,128)(2,1)} collective-permute-done((bf16[368,2048]{1,0:T(8,128)(2,1)}, bf16[368,2048]{1,0:T(8,128)(2,1)}, u32[]{:S(2)}, u32[]{:S(2)}) %collective-permute-start.13) | collective-permute-done | bytes 1507360 | tf_op jit(solution)/shard_map/ppermute | solution.py:315
  333.2 17.3 %conditional.1 = (bf16[1024,2048]{1,0:T(8,128)(2,1)}) conditional(s32[]{:T(128)} %bitcast.23, (s32[8,128]{1,0:T(8,128)}, s32[1024,8]{1,0:T(8,128)}, f32[1024,8]{1,0:T(8,128)}, bf16[368,2048]{1,0:T(8,128)(2,1)}, bf16[368,2048]{1,0:T(8,128)(2,1)}, /*index=5*/bf16[368,2048]{1,0:T(8,128)(2,1)}, bf16[368,2048]{1,0:T(8,128)(2,1)}, ...), branch_computations={%region_0.1_spmd, %region_1.5_spmd} | conditional | flops 22568288256 | bytes 176861824 | solution.py:360
  333.2 17.3 %branch_0_fun.1 = bf16[1024,2048]{1,0:T(8,128)(2,1)} custom-call(s32[8,128]{1,0:T(8,128)} %get-tuple-element.102.beg_ref, s32[1024,8]{1,0:T(8,128)} %get-tuple-element.103.pos_ref, f32[1024,8]{1,0:T(8,128)} %get-tuple-element.104.g_ref, bf16[368,2048]{1,0:T(8,128)(2,1)} %get-tuple-element.105.refs_0_, bf16[368,2048]{1,0:T(8,128)(2,1)} %get-tuple-element.106.refs_1_, ...), custom_call_target="tpu_custom_call" | custom-call | flops 8589934592 | bytes 28835840 | tf_op jit(solution)/shard_map/cond/branch_0_fun/pallas_call | solution.py:269
  (11 shorter events, 0.0 us)
Async XLA Ops:
  0.1 0.5 copy-start
  11.5 58.6 %collective-permute-start.1 = (bf16[368,2048]{1,0:T(8,128)(2,1)}, bf16[368,2048]{1,0:T(8,128)(2,1)}, u32[]{:S(2)}, u32[]{:S(2)}) collective-permute-start(bf16[368,2048]{1,0:T(8,128)(2,1)} %get-tuple-element.181), channel_id=1, source_target_pairs={{0,2},{1,3},{2,4},{3,5},{4,6},{5,7},{6,0},{7,1},{8,10},{9,11},{10,... | collective-permute-start | bytes 4521992 | tf_op jit(solution)/shard_map/ppermute | solution.py:315
  13.8 56.4 %collective-permute-start.2 = (bf16[368,2048]{1,0:T(8,128)(2,1)}, bf16[368,2048]{1,0:T(8,128)(2,1)}, u32[]{:S(2)}, u32[]{:S(2)}) collective-permute-start(bf16[368,2048]{1,0:T(8,128)(2,1)} %get-tuple-element.182), channel_id=1, source_target_pairs={{0,6},{1,7},{2,0},{3,1},{4,2},{5,3},{6,4},{7,5},{8,14},{9,15},{10,... | collective-permute-start | bytes 4521992 | tf_op jit(solution)/shard_map/ppermute | solution.py:315
  65.3 193.4 %collective-permute-start = (bf16[368,2048]{1,0:T(8,128)(2,1)}, bf16[368,2048]{1,0:T(8,128)(2,1)}, u32[]{:S(2)}, u32[]{:S(2)}) collective-permute-start(bf16[368,2048]{1,0:T(8,128)(2,1)} %get-tuple-element.178), channel_id=1, source_target_pairs={{0,1},{1,0},{2,3},{3,2},{4,5},{5,4},{6,7},{7,6},{8,9},{9,8},{10,11... | collective-permute-start | bytes 4521992 | tf_op jit(solution)/shard_map/ppermute | solution.py:315
  66.8 66.1 %collective-permute-start.5 = (bf16[368,2048]{1,0:T(8,128)(2,1)}, bf16[368,2048]{1,0:T(8,128)(2,1)}, u32[]{:S(2)}, u32[]{:S(2)}) collective-permute-start(bf16[368,2048]{1,0:T(8,128)(2,1)} %get-tuple-element.186), channel_id=1, source_target_pairs={{0,4},{1,5},{2,6},{3,7},{4,0},{5,1},{6,2},{7,3},{8,12},{9,13},{10,... | collective-permute-start | bytes 4521992 | tf_op jit(solution)/shard_map/ppermute | solution.py:315
  68.1 68.2 %collective-permute-start.6 = (bf16[368,2048]{1,0:T(8,128)(2,1)}, bf16[368,2048]{1,0:T(8,128)(2,1)}, u32[]{:S(2)}, u32[]{:S(2)}) collective-permute-start(bf16[368,2048]{1,0:T(8,128)(2,1)} %get-tuple-element.187), channel_id=1, source_target_pairs={{0,5},{1,4},{2,7},{3,6},{4,1},{5,0},{6,3},{7,2},{8,13},{9,12},{10,... | collective-permute-start | bytes 4521992 | tf_op jit(solution)/shard_map/ppermute | solution.py:315
  129.9 67.6 %collective-permute-start.3 = (bf16[368,2048]{1,0:T(8,128)(2,1)}, bf16[368,2048]{1,0:T(8,128)(2,1)}, u32[]{:S(2)}, u32[]{:S(2)}) collective-permute-start(bf16[368,2048]{1,0:T(8,128)(2,1)} %get-tuple-element.184), channel_id=1, source_target_pairs={{0,3},{1,2},{2,5},{3,4},{4,7},{5,6},{6,1},{7,0},{8,11},{9,10},{10,... | collective-permute-start | bytes 4521992 | tf_op jit(solution)/shard_map/ppermute | solution.py:315
  130.0 68.9 %collective-permute-start.4 = (bf16[368,2048]{1,0:T(8,128)(2,1)}, bf16[368,2048]{1,0:T(8,128)(2,1)}, u32[]{:S(2)}, u32[]{:S(2)}) collective-permute-start(bf16[368,2048]{1,0:T(8,128)(2,1)} %get-tuple-element.185), channel_id=1, source_target_pairs={{0,7},{1,6},{2,1},{3,0},{4,3},{5,2},{6,5},{7,4},{8,15},{9,14},{10,... | collective-permute-start | bytes 4521992 | tf_op jit(solution)/shard_map/ppermute | solution.py:315
  132.9 160.7 %collective-permute-start.8 = (bf16[368,2048]{1,0:T(8,128)(2,1)}, bf16[368,2048]{1,0:T(8,128)(2,1)}, u32[]{:S(2)}, u32[]{:S(2)}) collective-permute-start(bf16[368,2048]{1,0:T(8,128)(2,1)} %get-tuple-element.196), channel_id=1, source_target_pairs={{2,0},{3,1},{4,2},{5,3},{6,4},{7,5},{0,6},{1,7},{10,8},{11,9},{12,... | collective-permute-start | bytes 4521992 | tf_op jit(solution)/shard_map/ppermute | solution.py:315
  196.1 100.6 %collective-permute-start.10 = (bf16[368,2048]{1,0:T(8,128)(2,1)}, bf16[368,2048]{1,0:T(8,128)(2,1)}, u32[]{:S(2)}, u32[]{:S(2)}) collective-permute-start(bf16[368,2048]{1,0:T(8,128)(2,1)} %get-tuple-element.198), channel_id=1, source_target_pairs={{4,0},{5,1},{6,2},{7,3},{0,4},{1,5},{2,6},{3,7},{12,8},{13,9},{14,... | collective-permute-start | bytes 4521992 | tf_op jit(solution)/shard_map/ppermute | solution.py:315
  197.4 101.1 %collective-permute-start.11 = (bf16[368,2048]{1,0:T(8,128)(2,1)}, bf16[368,2048]{1,0:T(8,128)(2,1)}, u32[]{:S(2)}, u32[]{:S(2)}) collective-permute-start(bf16[368,2048]{1,0:T(8,128)(2,1)} %get-tuple-element.199), channel_id=1, source_target_pairs={{5,0},{4,1},{7,2},{6,3},{1,4},{0,5},{3,6},{2,7},{13,8},{12,9},{15,... | collective-permute-start | bytes 4521992 | tf_op jit(solution)/shard_map/ppermute | solution.py:315
  198.9 99.6 %collective-permute-start.12 = (bf16[368,2048]{1,0:T(8,128)(2,1)}, bf16[368,2048]{1,0:T(8,128)(2,1)}, u32[]{:S(2)}, u32[]{:S(2)}) collective-permute-start(bf16[368,2048]{1,0:T(8,128)(2,1)} %get-tuple-element.200), channel_id=1, source_target_pairs={{6,0},{7,1},{0,2},{1,3},{2,4},{3,5},{4,6},{5,7},{14,8},{15,9},{8,1... | collective-permute-start | bytes 4521992 | tf_op jit(solution)/shard_map/ppermute | solution.py:315
  293.0 5.6 %collective-permute-start.7 = (bf16[368,2048]{1,0:T(8,128)(2,1)}, bf16[368,2048]{1,0:T(8,128)(2,1)}, u32[]{:S(2)}, u32[]{:S(2)}) collective-permute-start(bf16[368,2048]{1,0:T(8,128)(2,1)} %get-tuple-element.195), channel_id=1, source_target_pairs={{1,0},{0,1},{3,2},{2,3},{5,4},{4,5},{7,6},{6,7},{9,8},{8,9},{11,10... | collective-permute-start | bytes 4521992 | tf_op jit(solution)/shard_map/ppermute | solution.py:315
  293.7 35.5 %collective-permute-start.9 = (bf16[368,2048]{1,0:T(8,128)(2,1)}, bf16[368,2048]{1,0:T(8,128)(2,1)}, u32[]{:S(2)}, u32[]{:S(2)}) collective-permute-start(bf16[368,2048]{1,0:T(8,128)(2,1)} %get-tuple-element.197), channel_id=1, source_target_pairs={{3,0},{2,1},{5,2},{4,3},{7,4},{6,5},{1,6},{0,7},{11,8},{10,9},{13,... | collective-permute-start | bytes 4521992 | tf_op jit(solution)/shard_map/ppermute | solution.py:315
  296.7 36.5 %collective-permute-start.13 = (bf16[368,2048]{1,0:T(8,128)(2,1)}, bf16[368,2048]{1,0:T(8,128)(2,1)}, u32[]{:S(2)}, u32[]{:S(2)}) collective-permute-start(bf16[368,2048]{1,0:T(8,128)(2,1)} %get-tuple-element.201), channel_id=1, source_target_pairs={{7,0},{6,1},{1,2},{0,3},{3,4},{2,5},{5,6},{4,7},{15,8},{14,9},{9,1... | collective-permute-start | bytes 4521992 | tf_op jit(solution)/shard_map/ppermute | solution.py:315
